TPU v7x, 32 devices: a whole 2x2x4 slice. The times are simulated.
32 devices in a mesh: genes: 16 (over z, y, core), cols: 2 (over x).
Axes of the slice: x: 2, y: 2, z: 4, core: 2. Of those that a mesh axis runs over, the one named last changes fastest.
Arguments:
- expression: float32 [384, 40960], P(None, ('genes', 'cols')), may hold values from -200 to 200
- resample: int32 [384], replicated, may hold values from 0 to 383
- labels: int32 [40960, 300], P(('genes', 'cols')), may hold values from 0 to 1, as said below
- ref_kim: float32 [40960], P(('genes', 'cols')), may hold values from 0 to 1
Outputs:
- connectivity: float32 [40960, 300], P(('genes', 'cols'))
- preservation: float32 [2, 300], replicated
Inputs may be any that keep to these rules, and one draw needn't show every extreme that they name: `labels`: each row holds exactly one 1; every module has 32 or more genes.
All inputs are finite; a program needn't handle non-finite values.
Results may differ from a plain program's by a relative error of at most 0.0031.
Values may be sent and summed in bfloat16 or wider, within the bound.
A program may use at most 128 MiB of HBM per device.

v0:
```python
import math
import jax
import jax.numpy as jnp
from jax import lax
from jax.sharding import PartitionSpec as P

G = 40960


def standardize(expression, resample):
    boot = jnp.take(expression, resample, axis=0)
    centered = boot - jnp.mean(boot, axis=0, keepdims=True)
    total = jnp.sum(centered * centered, axis=0, keepdims=True)
    return (centered * lax.rsqrt(total + 1e-06)).astype(jnp.bfloat16)


def local_sums(connectivity, labels, ref_kim):
    member = labels.astype(jnp.float32)
    kim = jnp.sum(connectivity * member, axis=1)
    rowsum = jnp.sum(connectivity, axis=1)
    stacked = jnp.stack(
        [kim, kim * kim, ref_kim, ref_kim * ref_kim, kim * ref_kim, rowsum, jnp.ones_like(kim)],
        axis=1,
    )
    return jnp.dot(
        member.T, stacked, precision=lax.Precision.HIGHEST, preferred_element_type=jnp.float32
    )


def preserve(sums, total_genes):
    counts = sums[:, 6]
    mean_x = sums[:, 0] / (counts * counts)
    var_x = jnp.maximum(sums[:, 1] / (counts * counts * counts) - mean_x * mean_x, 0.0001)
    mean_y = sums[:, 2] / counts
    var_y = jnp.maximum(sums[:, 3] / counts - mean_y * mean_y, 0.01)
    cross = sums[:, 4] / (counts * counts) - mean_x * mean_y
    between = (sums[:, 5] - sums[:, 0]) / (counts * (total_genes - counts))
    density = (mean_x - between) * jnp.sqrt(counts / var_x)
    linked = cross * jnp.sqrt(counts / (var_x * var_y))
    return jnp.stack([density, linked], axis=0)


def tile_term(row_block, column_block, column_ids, module_count):
    scores = lax.dot_general(
        row_block, column_block, (((0,), (0,)), ((), ())), preferred_element_type=jnp.float32
    )
    squares = scores * scores
    adjacency = (squares * squares * squares).astype(jnp.bfloat16)
    member_block = (
        column_ids[:, None] == jnp.arange(module_count, dtype=jnp.int32)[None, :]
    ).astype(jnp.bfloat16)
    return jnp.dot(adjacency, member_block, preferred_element_type=jnp.float32)


def add_tiles(carried, row_block, piece, every_ids, shard_width, module_count):
    span_width = piece.shape[1]
    column_step = shard_width * math.gcd(span_width // shard_width, 8)
    steps_total = span_width // column_step

    def one_step(step_index, accumulated):
        columns = lax.dynamic_slice_in_dim(piece, step_index * column_step, column_step, 1)
        column_ids = lax.dynamic_slice_in_dim(every_ids, step_index * column_step, column_step, 0)
        return accumulated + tile_term(row_block, columns, column_ids, module_count)

    return lax.fori_loop(0, steps_total, one_step, carried)


def local(expression, resample, labels, ref_kim):
    scaled = standardize(expression, resample)
    module_count = labels.shape[1]
    shard_width = scaled.shape[1]
    module_ids = jnp.sum(labels * jnp.arange(module_count, dtype=jnp.int32)[None, :], axis=1)
    row_block = lax.all_gather(scaled, "cols", axis=1, tiled=True)
    panel_ids = lax.all_gather(module_ids, "genes", axis=0, tiled=True)
    initial = jnp.zeros((row_block.shape[1], module_count), jnp.float32)
    partial_value = add_tiles(
        initial,
        row_block,
        lax.all_gather(scaled, "genes", axis=1, tiled=True),
        panel_ids,
        shard_width,
        module_count,
    )
    connectivity = lax.psum_scatter(partial_value, "cols", scatter_dimension=0, tiled=True)
    sums = lax.psum(local_sums(connectivity, labels, ref_kim), ("genes", "cols"))
    return (connectivity, preserve(sums, G))


def solution(mesh):
    placed = (P(None, ("genes", "cols")), P(), P(("genes", "cols"), None), P(("genes", "cols")))
    return jax.shard_map(
        local,
        mesh=mesh,
        in_specs=placed,
        out_specs=(P(("genes", "cols"), None), P()),
        check_vma=False,
    )
```

profile of v0, /device:TPU:0, one launch (start us, length us, event | category | flops | bytes accessed | tf_op | source)
XLA Modules:
  0.0 391.7 jit_solution(1327400909456358095)
XLA Ops:
  7.2 0.0 copy-start
  7.2 0.0 all-gather.6.cloned.1.call-start
  7.2 0.8 compare_select_fusion
  8.0 0.7 compare_and_fusion
  8.7 0.0 copy-done
  8.8 2.7 gather_fusion
  11.5 0.0 copy-start.2
  11.5 1.9 select_reduce_fusion
  13.4 0.2 copy-done.2
  13.6 0.3 multiply_reduce_fusion
  14.0 0.0 copy-start.3
  14.0 1.3 multiply_convert_fusion
  15.2 0.0 all-gather.6.cloned.1.call-update
  15.3 0.0 all-gather.4.cloned.1.call-start
  15.3 0.7 all-gather.4.cloned.1.call-update
  16.0 0.0 reduce-scatter.2.cloned.1.call-start
  16.1 0.0 copy-done.3
  16.1 0.2 multiply_reduce_fusion.2
  16.3 23.3 %all-gather = s32[16,1,1280]{2,1,0:T(1,128)S(1)} all-gather(s32[1,1,1280]{2,1,0:T(1,128)S(1)} %reshape.229), channel_id=1, replica_groups=mesh['genes'=16,'cols'=2] {'genes'}, dimensions={0}, use_global_device_ids=true | all-gather | bytes 87040 | tf_op jit(solution)/shard_map/all_gather | solution.py:74
  39.6 10.2 %all-gather.6.cloned.1.call-done = bf16[384,2560]{1,0:T(8,128)(2,1)} async-done(((bf16[384,1280]{1,0:T(8,128)(2,1)}), bf16[384,2560]{1,0:T(8,128)(2,1)}) %all-gather.6.cloned.1.call-update) | async-done | bytes 1966096 | tf_op jit(solution)/shard_map/all_gather | solution.py:73
  49.8 122.7 %all-gather.4.cloned.1.call-done = bf16[384,20480]{1,0:T(8,128)(2,1)} async-done(((bf16[384,1280]{1,0:T(8,128)(2,1)}), bf16[384,20480]{1,0:T(8,128)(2,1)}) %all-gather.4.cloned.1.call-update) | async-done | bytes 15728656 | tf_op jit(solution)/shard_map/all_gather | solution.py:79
  172.5 124.2 %while.14 = (s32[]{:T(128)}, f32[2560,300]{0,1:T(8,128)}, bf16[384,20480]{1,0:T(8,128)(2,1)}, bf16[384,2560]{1,0:T(8,128)(2,1)}, s32[20480]{0:T(1024)S(1)}, /*index=5*/s32[]{:T(128)}, s32[]{:T(128)}, s32[]{:T(128)}, s32[]{:T(128)}) while((s32[]{:T(128)}, f32[2560,300]{0,1:T(8,128)}, bf16[384,20480]{1,0:T(8,128)(2,1)}, ...), condition=%wide.region_4.5_spmd.clone, body=%wide.region_3.4_spmd.clone.sunk | while | flops 35970764800 | bytes 120955040 | solution.py:65
  172.5 37.4 %fusion.clone.9 = bf16[2560,10240]{0,1:T(8,128)(2,1)} fusion(bf16[384,2560]{1,0:T(8,128)(2,1)} %get-tuple-element.184, bf16[384,20480]{1,0:T(8,128)(2,1)} %get-tuple-element.183, s32[]{:T(128)S(6)} %select_n.27), kind=kOutput, calls=%fused_computation.2.clone.clone.clone.clone.clone.2.clone.1 | convolution fusion | flops 20237516800 | bytes 62259204 | tf_op jit(solution)/shard_map/while/body/eval_jaxpr/dot_general | solution.py:44
  209.9 24.2 %fusion.47 = f32[2560,300]{0,1:T(8,128)} fusion(s32[10240]{0:T(1024)S(1)} %dynamic_slice.28, f32[2560,300]{0,1:T(8,128)} %get-tuple-element.173, pred[]{:T(512)S(6)} %compare.3, bf16[2560,10240]{0,1:T(8,128)(2,1)} %fusion.clone.9), kind=kOutput, calls=%fused_computation.7.clone.3 | convolution fusion | flops 15733248000 | bytes 58613760 | tf_op jit(solution)/shard_map/while/body/eval_jaxpr/dot_general | solution.py:52
  234.1 37.4 %fusion.clone.9 = bf16[2560,10240]{0,1:T(8,128)(2,1)} fusion(bf16[384,2560]{1,0:T(8,128)(2,1)} %get-tuple-element.184, bf16[384,20480]{1,0:T(8,128)(2,1)} %get-tuple-element.183, s32[]{:T(128)S(6)} %select_n.27), kind=kOutput, calls=%fused_computation.2.clone.clone.clone.clone.clone.2.clone.1 | convolution fusion | flops 20237516800 | bytes 62259204 | tf_op jit(solution)/shard_map/while/body/eval_jaxpr/dot_general | solution.py:44
  271.6 25.1 %fusion.47 = f32[2560,300]{0,1:T(8,128)} fusion(s32[10240]{0:T(1024)S(1)} %dynamic_slice.28, f32[2560,300]{0,1:T(8,128)} %get-tuple-element.173, pred[]{:T(512)S(6)} %compare.3, bf16[2560,10240]{0,1:T(8,128)(2,1)} %fusion.clone.9), kind=kOutput, calls=%fused_computation.7.clone.3 | convolution fusion | flops 15733248000 | bytes 58613760 | tf_op jit(solution)/shard_map/while/body/eval_jaxpr/dot_general | solution.py:52
  296.7 0.0 copy-start.5
  296.7 0.0 copy-start.4
  296.7 0.0 reduce-scatter.2.cloned.1.call-update
  296.7 0.7 copy-done.5
  297.4 0.0 copy-start.1
  297.4 40.6 %reduce-scatter.2.cloned.1.call-done = f32[1280,300]{0,1:T(8,128)} async-done(((f32[2560,300]{0,1:T(8,128)}), f32[1280,300]{0,1:T(8,128)}) %reduce-scatter.2.cloned.1.call-update) | async-done | bytes 1536016 | tf_op jit(solution)/shard_map/reduce_scatter | solution.py:84
  338.0 0.0 copy-done.4
  338.0 1.6 fusion.26
  339.7 0.6 stack.27
  340.3 0.6 stack.28
  340.9 0.6 stack_broadcast_in_dim.3
  341.5 1.4 stack.29
  342.9 2.1 fusion.12
  345.0 39.5 %psum.7 = f32[300,7]{0,1:T(8,128)S(1)} all-reduce(f32[300,7]{0,1:T(8,128)S(1)} %fusion.12), channel_id=1, replica_groups=mesh['genes'=16,'cols'=2] {'genes','cols'}, use_global_device_ids=true, to_apply=%region_8.9 | all-reduce | flops 2100 | bytes 16800 | tf_op jit(solution)/shard_map/psum | solution.py:85
  384.6 0.6 pad_maximum_fusion
  385.1 0.0 copy-done.1
  (14 shorter events, 0.1 us)
Async XLA Ops:
  7.2 1.6 copy-start
  7.2 42.6 %all-gather.6.cloned.1.call-start = ((), (), s32[]{:S(2)}) async-start(), calls=%async_computation.2 | async-start | bytes 2949120 | tf_op jit(solution)/shard_map/all_gather | solution.py:73
  11.5 2.1 copy-start.2
  14.0 2.1 copy-start.3
  15.3 157.2 %all-gather.4.cloned.1.call-start = ((), (), s32[]{:S(2)}) async-start(), calls=%async_computation.1 | async-start | bytes 16711680 | tf_op jit(solution)/shard_map/all_gather | solution.py:79
  16.0 322.0 %reduce-scatter.2.cloned.1.call-start = ((), (), s32[]{:S(2)}) async-start(), calls=%async_computation.3 | async-start | bytes 4669440 | tf_op jit(solution)/shard_map/reduce_scatter | solution.py:84
  296.7 0.7 copy-start.5
  296.7 41.4 %copy-start.4 = (s32[1280,300]{0,1:T(8,128)S(1)}, s32[1280,300]{0,1:T(8,128)}, u32[]{:S(2)}) copy-start(s32[1280,300]{0,1:T(8,128)} %param.8) | copy-start | bytes 4608004
  297.4 87.8 %copy-start.1 = (f32[384,1280]{1,0:T(8,128)S(1)}, f32[384,1280]{1,0:T(8,128)}, u32[]{:S(2)}) copy-start(f32[384,1280]{1,0:T(8,128)} %param.6) | copy-start | bytes 5898244
Sparse Core Ops, SparseCore 0:
  15.4 34.3 all-gather.5
  52.6 119.7 all-gather.3
  296.8 41.1 reduce-scatter.1
where the time goes:
time: 392 us
  waiting for transfers between devices  174 us (44%)
  matrix products  126 us (32%)
  blocking collectives  62.8 us (16%)
  between operations  13.9 us (4%)
  other arithmetic  7.47 us (2%)
  local copies, waits for them, and re-layouts  6.83 us (2%)
    all_gather x1, waiting for transfers between devices, local(): lax.all_gather(scaled, 'genes', axis=1, tiled=True)  123 us
    dot_general x2, matrix products, tile_term(): lax.dot_general(row_block, column_block, (((0,), (0,)), ((), ())), prefer...  74.9 us
    dot_general x2, matrix products, tile_term(): return jnp.dot(adjacency, member_block, preferred_element_type=jnp.float32)  49.3 us
    reduce_scatter x1, waiting for transfers between devices, local(): lax.psum_scatter(partial_value, 'cols', scatter_dimension=0, tiled=True)  40.6 us
    psum x1, blocking collectives, local(): lax.psum(local_sums(connectivity, labels, ref_kim), ('genes', 'cols'))  39.5 us
    all_gather x1, blocking collectives, local(): panel_ids = lax.all_gather(module_ids, 'genes', axis=0, tiled=True)  23.3 us
    all_gather x1, waiting for transfers between devices, local(): row_block = lax.all_gather(scaled, 'cols', axis=1, tiled=True)  10.2 us
  transfers between devices with their start and end apart: 3, of which 3 were waited for; matrix products, arithmetic and copies ran while one was open for 0% of the time, Pallas kernels for 0%

commit v1 on v0

--- a/solution.py
+++ b/solution.py
@@ -3,6 +3,7 @@
 import jax.numpy as jnp
 from jax import lax
 from jax.sharding import PartitionSpec as P
+from jax.lax import all_gather
 
 G = 40960
 
@@ -82,7 +83,8 @@
         module_count,
     )
     connectivity = lax.psum_scatter(partial_value, "cols", scatter_dimension=0, tiled=True)
-    sums = lax.psum(local_sums(connectivity, labels, ref_kim), ("genes", "cols"))
+    inner_x = local_sums(connectivity, labels, ref_kim)
+    sums = jnp.sum(all_gather(inner_x, ("genes", "cols")), 0)
     return (connectivity, preserve(sums, G))
 
 

time: 392 us -> 422 us (1.077)
  blocking collectives: 62.8 us -> 92.2 us
    all_gather x0 -> x1, blocking collectives: none -> 68.9 us  [local(): sums = jnp.sum(all_gather(inner_x, ('genes', 'cols')), 0)]
    psum x1 -> x0, blocking collectives: 39.5 us -> none  [local(): lax.psum(local_sums(connectivity, labels, ref_kim), ('genes', 'cols'))]
where the time goes in v1:
time: 422 us; the launch traced here: 421 us
  waiting for transfers between devices  174 us (41%)
  matrix products  126 us (30%)
  blocking collectives  92.2 us (22%)
  between operations  13.9 us (3%)
  other arithmetic  7.66 us (2%)
  local copies, waits for them, and re-layouts  6.83 us (2%)
    all_gather x1, waiting for transfers between devices, local(): lax.all_gather(scaled, 'genes', axis=1, tiled=True)  123 us
    dot_general x2, matrix products, tile_term(): lax.dot_general(row_block, column_block, (((0,), (0,)), ((), ())), prefer...  74.9 us
    all_gather x1, blocking collectives, local(): sums = jnp.sum(all_gather(inner_x, ('genes', 'cols')), 0)  68.9 us
    dot_general x2, matrix products, tile_term(): return jnp.dot(adjacency, member_block, preferred_element_type=jnp.float32)  49.3 us
    reduce_scatter x1, waiting for transfers between devices, local(): lax.psum_scatter(partial_value, 'cols', scatter_dimension=0, tiled=True)  40.7 us
    all_gather x1, blocking collectives, local(): panel_ids = lax.all_gather(module_ids, 'genes', axis=0, tiled=True)  23.3 us
    all_gather x1, waiting for transfers between devices, local(): row_block = lax.all_gather(scaled, 'cols', axis=1, tiled=True)  10.2 us
  transfers between devices with their start and end apart: 3, of which 3 were waited for; matrix products, arithmetic and copies ran while one was open for 0% of the time, Pallas kernels for 0%

profile of v1, /device:TPU:0, one launch (start us, length us, event | category | flops | bytes accessed | tf_op | source)
XLA Modules:
  0.0 421.3 jit_solution(4930236860352579865)
XLA Ops:
  7.2 0.0 copy-start
  7.2 0.0 all-gather.8.cloned.1.call-start
  7.2 0.8 compare_select_fusion
  8.0 0.7 compare_and_fusion
  8.7 0.0 copy-done
  8.8 2.7 gather_fusion
  11.5 0.0 copy-start.2
  11.5 1.9 select_reduce_fusion
  13.4 0.2 copy-done.2
  13.6 0.3 multiply_reduce_fusion
  14.0 0.0 copy-start.3
  14.0 1.3 multiply_convert_fusion
  15.2 0.0 all-gather.8.cloned.1.call-update
  15.3 0.0 all-gather.6.cloned.1.call-start
  15.3 0.7 all-gather.6.cloned.1.call-update
  16.0 0.0 reduce-scatter.2.cloned.1.call-start
  16.1 0.0 copy-done.3
  16.1 0.2 multiply_reduce_fusion.2
  16.3 23.3 %all-gather.1 = s32[16,1,1280]{2,1,0:T(1,128)S(1)} all-gather(s32[1,1,1280]{2,1,0:T(1,128)S(1)} %reshape.230), channel_id=1, replica_groups=mesh['genes'=16,'cols'=2] {'genes'}, dimensions={0}, use_global_device_ids=true | all-gather | bytes 87040 | tf_op jit(solution)/shard_map/all_gather | solution.py:75
  39.6 10.2 %all-gather.8.cloned.1.call-done = bf16[384,2560]{1,0:T(8,128)(2,1)} async-done(((bf16[384,1280]{1,0:T(8,128)(2,1)}), bf16[384,2560]{1,0:T(8,128)(2,1)}) %all-gather.8.cloned.1.call-update) | async-done | bytes 1966096 | tf_op jit(solution)/shard_map/all_gather | solution.py:74
  49.8 122.7 %all-gather.6.cloned.1.call-done = bf16[384,20480]{1,0:T(8,128)(2,1)} async-done(((bf16[384,1280]{1,0:T(8,128)(2,1)}), bf16[384,20480]{1,0:T(8,128)(2,1)}) %all-gather.6.cloned.1.call-update) | async-done | bytes 15728656 | tf_op jit(solution)/shard_map/all_gather | solution.py:80
  172.5 124.2 %while.14 = (s32[]{:T(128)}, f32[2560,300]{0,1:T(8,128)}, bf16[384,20480]{1,0:T(8,128)(2,1)}, bf16[384,2560]{1,0:T(8,128)(2,1)}, s32[20480]{0:T(1024)S(1)}, /*index=5*/s32[]{:T(128)}, s32[]{:T(128)}, s32[]{:T(128)}, s32[]{:T(128)}) while((s32[]{:T(128)}, f32[2560,300]{0,1:T(8,128)}, bf16[384,20480]{1,0:T(8,128)(2,1)}, ...), condition=%wide.region_4.5_spmd.clone, body=%wide.region_3.4_spmd.clone.sunk | while | flops 35970764800 | bytes 120955040 | solution.py:66
  172.5 37.4 %fusion.clone.9 = bf16[2560,10240]{0,1:T(8,128)(2,1)} fusion(bf16[384,2560]{1,0:T(8,128)(2,1)} %get-tuple-element.184, bf16[384,20480]{1,0:T(8,128)(2,1)} %get-tuple-element.183, s32[]{:T(128)S(6)} %select_n.27), kind=kOutput, calls=%fused_computation.2.clone.clone.clone.clone.clone.2.clone.1 | convolution fusion | flops 20237516800 | bytes 62259204 | tf_op jit(solution)/shard_map/while/body/eval_jaxpr/dot_general | solution.py:45
  209.9 24.2 %fusion.47 = f32[2560,300]{0,1:T(8,128)} fusion(s32[10240]{0:T(1024)S(1)} %dynamic_slice.28, f32[2560,300]{0,1:T(8,128)} %get-tuple-element.173, pred[]{:T(512)S(6)} %compare.3, bf16[2560,10240]{0,1:T(8,128)(2,1)} %fusion.clone.9), kind=kOutput, calls=%fused_computation.7.clone.3 | convolution fusion | flops 15733248000 | bytes 58613760 | tf_op jit(solution)/shard_map/while/body/eval_jaxpr/dot_general | solution.py:53
  234.1 37.4 %fusion.clone.9 = bf16[2560,10240]{0,1:T(8,128)(2,1)} fusion(bf16[384,2560]{1,0:T(8,128)(2,1)} %get-tuple-element.184, bf16[384,20480]{1,0:T(8,128)(2,1)} %get-tuple-element.183, s32[]{:T(128)S(6)} %select_n.27), kind=kOutput, calls=%fused_computation.2.clone.clone.clone.clone.clone.2.clone.1 | convolution fusion | flops 20237516800 | bytes 62259204 | tf_op jit(solution)/shard_map/while/body/eval_jaxpr/dot_general | solution.py:45
  271.6 25.1 %fusion.47 = f32[2560,300]{0,1:T(8,128)} fusion(s32[10240]{0:T(1024)S(1)} %dynamic_slice.28, f32[2560,300]{0,1:T(8,128)} %get-tuple-element.173, pred[]{:T(512)S(6)} %compare.3, bf16[2560,10240]{0,1:T(8,128)(2,1)} %fusion.clone.9), kind=kOutput, calls=%fused_computation.7.clone.3 | convolution fusion | flops 15733248000 | bytes 58613760 | tf_op jit(solution)/shard_map/while/body/eval_jaxpr/dot_general | solution.py:53
  296.7 0.0 copy-start.5
  296.7 0.0 copy-start.4
  296.7 0.0 reduce-scatter.2.cloned.1.call-update
  296.7 0.7 copy-done.5
  297.4 40.7 %reduce-scatter.2.cloned.1.call-done = f32[1280,300]{0,1:T(8,128)} async-done(((f32[2560,300]{0,1:T(8,128)}), f32[1280,300]{0,1:T(8,128)}) %reduce-scatter.2.cloned.1.call-update) | async-done | bytes 1536016 | tf_op jit(solution)/shard_map/reduce_scatter | solution.py:85
  338.1 0.0 copy-done.4
  338.1 0.0 copy-start.1
  338.1 1.8 fusion.26
  339.9 0.6 stack.27
  340.5 0.6 stack.28
  341.1 0.6 stack_broadcast_in_dim.3
  341.7 1.4 stack.29
  343.1 2.1 fusion.12
  345.2 68.9 %all-gather.2 = f32[32,300,7]{1,2,0:T(8,128)S(1)} all-gather(f32[1,300,7]{1,2,0:T(8,128)S(1)} %fusion.12), channel_id=2, replica_groups=mesh['genes'=16,'cols'=2] {'genes','cols'}, dimensions={0}, use_global_device_ids=true | all-gather | bytes 277200 | tf_op jit(solution)/shard_map/all_gather | solution.py:87
  414.2 0.6 pad_maximum_fusion
  414.8 0.0 copy-done.1
  (15 shorter events, 0.2 us)
Async XLA Ops:
  7.2 1.6 copy-start
  7.2 42.6 %all-gather.8.cloned.1.call-start = ((), (), s32[]{:S(2)}) async-start(), calls=%async_computation.2 | async-start | bytes 2949120 | tf_op jit(solution)/shard_map/all_gather | solution.py:74
  11.5 2.1 copy-start.2
  14.0 2.1 copy-start.3
  15.3 157.2 %all-gather.6.cloned.1.call-start = ((), (), s32[]{:S(2)}) async-start(), calls=%async_computation.1 | async-start | bytes 16711680 | tf_op jit(solution)/shard_map/all_gather | solution.py:80
  16.0 322.1 %reduce-scatter.2.cloned.1.call-start = ((), (), s32[]{:S(2)}) async-start(), calls=%async_computation.3 | async-start | bytes 4669440 | tf_op jit(solution)/shard_map/reduce_scatter | solution.py:85
  296.7 0.7 copy-start.5
  296.7 41.4 %copy-start.4 = (s32[1280,300]{0,1:T(8,128)S(1)}, s32[1280,300]{0,1:T(8,128)}, u32[]{:S(2)}) copy-start(s32[1280,300]{0,1:T(8,128)} %param.8) | copy-start | bytes 4608004
  338.1 76.7 %copy-start.1 = (f32[384,1280]{1,0:T(8,128)S(1)}, f32[384,1280]{1,0:T(8,128)}, u32[]{:S(2)}) copy-start(f32[384,1280]{1,0:T(8,128)} %param.6) | copy-start | bytes 5898244
Sparse Core Ops, SparseCore 0:
  15.4 34.3 all-gather.7
  52.6 119.7 all-gather.5
  296.8 41.1 reduce-scatter.1
